TPU v7x, 32 devices: a whole 2x2x4 slice. The times are simulated.
32 devices in a mesh: tm: 4 (over x, core), env: 8 (over z, y).
Axes of the slice: x: 2, y: 2, z: 4, core: 2. Of those that a mesh axis runs over, the one named last changes fastest.
Arguments:
- rewards: float32 [2048, 4096], P('tm', 'env'), may hold values from -0.4 to 0.4
- values: float32 [2048, 4096], P('tm', 'env'), may hold values from -0.4 to 0.4
- done_flags: int32 [2048, 4096], P('tm', 'env'), may hold values 0 or 1
- bootstrap: float32 [4096], P('env'), may hold values from -0.4 to 0.4
- discount_horizon: float32 [4096], P('env'), may hold values from 10 to 16384
- trace_horizon: float32 [4096], P('env'), may hold values from 10 to 16384
Outputs:
- norm_advantage: float32 [2048, 4096], P('tm', 'env')
- return_target: float32 [2048, 4096], P('tm', 'env')
All inputs are finite; a program needn't handle non-finite values. No bound on the sum of `done_flags` on one device may be relied on, other than what follows from the above.
Results may differ from a plain program's by a relative error of at most 0.0003.
Values sent between devices are 32-bit elements; how exact they have to be, the bound alone decides.
No kernel may reach another device: no remote copies, remote signals or barrier semaphores. Data moves between devices by JAX's collectives and lax.ppermute only.
A program may use at most 64 MiB of HBM per device.

v0:
```python
import functools

import jax
import jax.numpy as jnp
from jax import lax
from jax.experimental import pallas as pl
from jax.experimental.pallas import tpu as pltpu
from jax.sharding import PartitionSpec as P

LANES = 128
SUBS = 8
F32 = jnp.float32


def spread(row):
    return jnp.broadcast_to(row, (SUBS, row.shape[1]))


def scan_kernel(r_ref, v_ref, d_ref, dh_ref, th_ref, g_ref, p_ref, tot_ref, carry, acc):
    step = pl.program_id(0)
    rows, width = r_ref.shape

    @pl.when(step == 0)
    def _():
        carry[0] = jnp.zeros((SUBS, width), F32)
        carry[1] = jnp.ones((SUBS, width), F32)
        acc[...] = jnp.zeros(acc.shape, F32)

    sub = lax.broadcasted_iota(jnp.int32, (SUBS, LANES), 0)
    masks = {k: sub < SUBS - k for k in (1, 2, 4)}
    for c in range(width // LANES):
        at = pl.ds(c * LANES, LANES)
        trace = 1.0 - 1.0 / th_ref[:, at]
        rate = (1.0 - 1.0 / dh_ref[:, at]) * trace
        inv = 1.0 / trace
        rate, inv, extra = spread(rate), spread(inv), spread(inv - 1.0)
        z_in, p_in = carry[0, :, at], carry[1, :, at]
        sums = [acc[i, :, at] for i in range(5)]
        for j in reversed(range(rows // SUBS)):
            rs = pl.ds(j * SUBS, SUBS)
            v = v_ref[rs, at]
            u = r_ref[rs, at] + v * extra
            a = jnp.where(d_ref[rs, at] != 0, 0.0, rate)
            for k in (1, 2, 4):
                m = masks[k]
                u = u + jnp.where(m, a, 0.0) * pltpu.roll(u, SUBS - k, 0)
                a = a * jnp.where(m, pltpu.roll(a, SUBS - k, 0), 1.0)
            g = u + a * z_in - v * inv
            p = a * p_in
            z_in = spread(u[0:1]) + spread(a[0:1]) * z_in
            p_in = spread(a[0:1]) * p_in
            g_ref[rs, at] = g
            p_ref[rs, at] = p
            sums = [sums[0] + p, sums[1] + g * p, sums[2] + p * p, sums[3] + g, sums[4] + g * g]
        carry[0, :, at] = z_in
        carry[1, :, at] = p_in
        for i in range(5):
            acc[i, :, at] = sums[i]

    @pl.when(step == pl.num_programs(0) - 1)
    def _():
        tot_ref[0:1] = carry[1, 0:1]
        tot_ref[1:2] = carry[0, 0:1]
        for i in range(5):
            tot_ref[2 + i:3 + i] = jnp.sum(acc[i], axis=0, keepdims=True)
        tot_ref[7:8] = jnp.zeros((1, width), F32)


def pair_kernel(at_ref, mine_ref, other_ref, boot_ref, th_ref, send_ref, aux_ref, *, slots, copies):
    width = mine_ref.shape[1]
    half = width // 2
    m = half // LANES
    odd, last = at_ref[0], at_ref[1]
    late_here = odd == 1
    mine, other = mine_ref[...], other_ref[...]
    late = jnp.where(late_here, mine, other)
    early = jnp.where(late_here, other, mine)
    la, lz, lp, lgp, lpp, lg, lgg = [late[i:i + 1] for i in range(7)]
    ea, ez, ep, egp, epp, eg, egg = [early[i:i + 1] for i in range(7)]
    a, z = la * ea, ez + ea * lz
    p = lp + ep * la
    gp = lgp + (egp + epp * lz) * la
    pp = lpp + epp * la * la
    g = lg + eg + ep * lz
    gg = lgg + egg + (2.0 * egp + epp * lz) * lz
    known = boot_ref[...] / (1.0 - 1.0 / th_ref[...])
    is_last = last == 1
    g_end = g + p * known
    gg_end = gg + (2.0 * gp + pp * known) * known
    z_end = z + a * known
    g = jnp.where(is_last, g_end, g)
    gg = jnp.where(is_last, gg_end, gg)
    if slots == 3:
        parts = [jnp.where(is_last, z_end, p), gp, pp]
    else:
        parts = [jnp.where(is_last, z_end, z), p, gp, pp, a]
    mult = jnp.where(late_here, jnp.ones_like(la), la)
    add = jnp.where(late_here, jnp.zeros_like(la), lz)
    aux_ref[0:1] = jnp.where(is_last, 0.0, mult)
    aux_ref[1:2] = jnp.where(is_last, add + mult * known, add)
    aux_ref[2:8] = jnp.zeros((6, width), F32)

    def own(x):
        return jnp.where(late_here, x[:, half:], x[:, :half])

    rows = []
    for part in parts:
        h = own(part)
        rows += [h[:, i * LANES:(i + 1) * LANES] for i in range(m)]
    for total in (g, gg):
        h = own(total)
        rows.append(sum(h[:, i * LANES:(i + 1) * LANES] for i in range(m)))
    block = jnp.concatenate(rows, axis=0)
    send_ref[...] = jnp.broadcast_to(block[None], (copies,) + block.shape)


def finish_kernel(at_ref, got_ref, aux_ref, v_ref, g_ref, p_ref, norm_ref, ret_ref, z_ref, st_ref,
                  *, slots, pairs, groups, cells):
    rows, width = v_ref.shape
    half = width // 2
    m = half // LANES

    @pl.when(pl.program_id(0) == 0)
    def _():
        pair, group = at_ref[2], at_ref[3]
        n = 2 * groups
        base = slots * m
        got = [got_ref[k * n:(k + 1) * n] for k in range(pairs)]
        s1 = sum(jnp.sum(x[:, base:base + 1], axis=0) for x in got)
        s2 = sum(jnp.sum(x[:, base + 1:base + 2], axis=0) for x in got)
        off = 0 if slots == 3 else m
        z = got[pairs - 1][:, 0:m]
        here = [got_ref[(pairs - 1) * n + core * groups + group, 0:m] for core in range(2)]
        pick = here
        for k in reversed(range(pairs - 1)):
            x = got[k]
            p, gp, pp = [x[:, off + i * m:off + (i + 1) * m] for i in range(3)]
            t1 = jnp.sum(p * z, axis=0)
            t2 = jnp.sum((2.0 * gp + pp * z) * z, axis=0)
            s1 = s1 + jnp.sum(t1, axis=0, keepdims=True)
            s2 = s2 + jnp.sum(t2, axis=0, keepdims=True)
            pick = [jnp.where(pair == k, b, a) for a, b in zip(pick, here)]
            if k:
                z = x[:, 0:m] + x[:, 4 * m:5 * m] * z
                nxt = [got_ref[k * n + core * groups + group] for core in range(2)]
                here = [y[0:m] + y[4 * m:5 * m] * h for y, h in zip(nxt, here)]
        flat = jnp.concatenate([h[i:i + 1] for h in pick for i in range(m)], axis=1)
        z_in = aux_ref[1:2] + aux_ref[0:1] * flat
        mean = jnp.sum(s1, axis=1, keepdims=True) / cells
        var = jnp.sum(s2, axis=1, keepdims=True) / cells - mean * mean
        scale = 1.0 / jnp.sqrt(var + 1.0)
        z_ref[...] = spread(z_in)
        st_ref[0] = jnp.broadcast_to(mean, (SUBS, LANES))
        st_ref[1] = jnp.broadcast_to(scale, (SUBS, LANES))

    mean, scale = st_ref[0], st_ref[1]
    for c in range(width // LANES):
        at = pl.ds(c * LANES, LANES)
        z_in = z_ref[:, at]
        for j in range(rows // SUBS):
            rs = pl.ds(j * SUBS, SUBS)
            adv = g_ref[rs, at] + p_ref[rs, at] * z_in
            norm_ref[rs, at] = (adv - mean) * scale
            ret_ref[rs, at] = adv + v_ref[rs, at]


def local(rewards, values, done_flags, bootstrap, discount_horizon, trace_horizon):
    rows, width = rewards.shape
    blocks, groups = lax.axis_size("tm"), lax.axis_size("env")
    pairs, devices = blocks // 2, blocks * groups
    slots = 3 if pairs == 2 else 5
    m = width // 2 // LANES
    block_at, group = lax.axis_index("tm"), lax.axis_index("env")
    place = jnp.stack([block_at % 2, (block_at // 2 == pairs - 1).astype(jnp.int32), block_at // 2, group]).astype(jnp.int32)
    boot, dh, th = bootstrap[None], discount_horizon[None], trace_horizon[None]

    steps = 4
    part = rows // steps
    back = pl.BlockSpec((part, width), lambda i: (steps - 1 - i, 0))
    fore = pl.BlockSpec((part, width), lambda i: (i, 0))
    row = pl.BlockSpec((1, width), lambda i: (0, 0))
    eight = pl.BlockSpec((SUBS, width), lambda i: (0, 0))
    full = jax.ShapeDtypeStruct((rows, width), F32)
    gain, weight, totals = pl.pallas_call(
        scan_kernel,
        grid=(steps,),
        in_specs=[back, back, back, row, row],
        out_specs=[back, back, eight],
        out_shape=[full, full, jax.ShapeDtypeStruct((SUBS, width), F32)],
        scratch_shapes=[pltpu.VMEM((2, SUBS, width), F32), pltpu.VMEM((5, SUBS, width), F32)],
        name="scan",
    )(rewards, values, done_flags, dh, th)

    other = lax.ppermute(totals, "tm", [(i, i ^ 1) for i in range(blocks)])
    packed = slots * m + 2
    vmem = pl.BlockSpec(memory_space=pltpu.VMEM)
    smem = pl.BlockSpec(memory_space=pltpu.SMEM)
    send, aux = pl.pallas_call(
        functools.partial(pair_kernel, slots=slots, copies=devices),
        in_specs=[smem, vmem, vmem, vmem, vmem],
        out_specs=[vmem, vmem],
        out_shape=[jax.ShapeDtypeStruct((devices, packed, LANES), F32), jax.ShapeDtypeStruct((SUBS, width), F32)],
        name="pair",
    )(place, totals, other, boot, th)
    got = lax.all_to_all(send, ("tm", "env"), 0, 0, tiled=True)

    whole = pl.BlockSpec((devices, packed, LANES), lambda i: (0, 0, 0))
    return tuple(pl.pallas_call(
        functools.partial(finish_kernel, slots=slots, pairs=pairs, groups=groups,
                          cells=1.0 * rows * width * devices),
        grid=(steps,),
        in_specs=[smem, whole, eight, fore, fore, fore],
        out_specs=[fore, fore],
        out_shape=[full, full],
        scratch_shapes=[pltpu.VMEM((SUBS, width), F32), pltpu.VMEM((2, SUBS, LANES), F32)],
        name="finish",
    )(place, got, aux, values, gain, weight))


def solution(mesh):
    placed = (P("tm", "env"), P("tm", "env"), P("tm", "env"), P("env"), P("env"), P("env"))
    return jax.shard_map(
        local,
        mesh=mesh,
        in_specs=placed,
        out_specs=(P("tm", "env"), P("tm", "env")),
        check_vma=False,
    )
```

profile of v0, /device:TPU:0, one launch (start us, length us, event | category | flops | bytes accessed | tf_op | source)
XLA Modules:
  0.0 28.5 jit_solution(17251344025189966394)
XLA Ops:
  0.6 4.7 %scan.1 = (f32[512,512]{1,0:T(8,128)}, f32[512,512]{1,0:T(8,128)}, f32[8,512]{1,0:T(8,128)}) custom-call(f32[512,512]{1,0:T(8,128)} %r_ref.1, f32[512,512]{1,0:T(8,128)} %v_ref.3, s32[512,512]{1,0:T(8,128)} %d_ref.1, f32[1,512]{1,0:T(1,128)} %bitcast.9, f32[1,512]{1,0:T(1,128)} %bitcast.7), custom_call_target="tpu_custom_call" | custom-call | tf_op jit(solution)/shard_map/scan/pallas_call | solution.py:184
  5.3 0.6 %collective-permute-start = (f32[8,512]{1,0:T(8,128)}, f32[8,512]{1,0:T(8,128)S(1)}, u32[]{:S(2)}, u32[]{:S(2)}) collective-permute-start(f32[8,512]{1,0:T(8,128)} %get-tuple-element.7.mine_ref), channel_id=1, source_target_pairs={{0,8},{8,0},{16,24},{24,16},{1,9},{9,1},{17,25},{25,17},{2,10},{10... | collective-permute-start | bytes 49160 | tf_op jit(solution)/shard_map/ppermute | solution.py:194
  5.9 0.6 %pad_add_fusion.at_ref = s32[4]{0:T(128)} fusion(s32[1]{0:T(128)} %bitcast.3, s32[1]{0:T(128)} %bitcast.2, s32[1]{0:T(128)} %bitcast.1, s32[1]{0:T(128)} %bitcast), kind=kLoop, calls=%fused_computation | loop fusion | flops 12 | bytes 32 | tf_op jit(solution)/shard_map/stack | solution.py:174
  6.4 0.5 %collective-permute-done.other_ref = f32[8,512]{1,0:T(8,128)S(1)} collective-permute-done((f32[8,512]{1,0:T(8,128)}, f32[8,512]{1,0:T(8,128)S(1)}, u32[]{:S(2)}, u32[]{:S(2)}) %collective-permute-start) | collective-permute-done | bytes 16416 | tf_op jit(solution)/shard_map/ppermute | solution.py:194
  6.9 0.0 copy-start
  6.9 0.6 %copy-done = f32[8,512]{1,0:T(8,128)} copy-done((f32[8,512]{1,0:T(8,128)}, f32[8,512]{1,0:T(8,128)S(1)}, u32[]{:S(2)}) %copy-start) | copy-done | bytes 16408
  7.5 1.5 %pair.1 = (f32[32,8,128]{2,1,0:T(8,128)}, f32[8,512]{1,0:T(8,128)}) custom-call(s32[4]{0:T(128)} %pad_add_fusion.at_ref, f32[8,512]{1,0:T(8,128)} %get-tuple-element.7.mine_ref, f32[8,512]{1,0:T(8,128)} %copy-done, f32[1,512]{1,0:T(1,128)} %bitcast.10, f32[1,512]{1,0:T(1,128)} %bitcast.8), custom_call_target="tpu_custom_call" | custom-call | tf_op jit(solution)/shard_map/pair/pallas_call | solution.py:198
  9.0 15.1 %all_to_all.5.got_ref = f32[32,8,128]{2,1,0:T(8,128)} all-to-all(f32[32,8,128]{2,1,0:T(8,128)} %get-tuple-element.8), channel_id=1, replica_groups=mesh['tm'=4,'env'=8] {'tm','env'}, dimensions={0} | all-to-all | bytes 262144 | tf_op jit(solution)/shard_map/all_to_all | solution.py:205
  24.1 4.3 %finish.1 = (f32[512,512]{1,0:T(8,128)}, f32[512,512]{1,0:T(8,128)}) custom-call(s32[4]{0:T(128)} %pad_add_fusion.at_ref, f32[32,8,128]{2,1,0:T(8,128)} %all_to_all.5.got_ref, f32[8,512]{1,0:T(8,128)} %get-tuple-element.9.aux_ref, f32[512,512]{1,0:T(8,128)} %v_ref.3, f32[512,512]{1,0:T(8,128)} %get-tuple-element.10.g_ref, f32[512,512]{1,0:T(8,128)} %get-tuple-element.11.p_ref), custom_call_target="tpu_custom_call" | custom-call | tf_op jit(solution)/shard_map/finish/pallas_call | solution.py:208
Async XLA Ops:
  5.3 1.6 %collective-permute-start = (f32[8,512]{1,0:T(8,128)}, f32[8,512]{1,0:T(8,128)S(1)}, u32[]{:S(2)}, u32[]{:S(2)}) collective-permute-start(f32[8,512]{1,0:T(8,128)} %get-tuple-element.7.mine_ref), channel_id=1, source_target_pairs={{0,8},{8,0},{16,24},{24,16},{1,9},{9,1},{17,25},{25,17},{2,10},{10... | collective-permute-start | bytes 49160 | tf_op jit(solution)/shard_map/ppermute | solution.py:194
  6.9 0.6 %copy-start = (f32[8,512]{1,0:T(8,128)}, f32[8,512]{1,0:T(8,128)S(1)}, u32[]{:S(2)}) copy-start(f32[8,512]{1,0:T(8,128)S(1)} %collective-permute-done.other_ref) | copy-start | bytes 49156
where the time goes:
time: 28.8 us; the launch traced here: 28.5 us
  blocking collectives  15.1 us (52%)
  Pallas kernels  10.5 us (36%)
  between operations  0.63 us (2%)
  local copies, waits for them, and re-layouts  0.6 us (2%)
  starting transfers between devices  0.56 us (2%)
  other arithmetic  0.56 us (2%)
  waiting for transfers between devices  0.49 us (2%)
    all_to_all x1, blocking collectives, local(): got = lax.all_to_all(send, ('tm', 'env'), 0, 0, tiled=True)  15.1 us
    pallas_call x1, Pallas kernels, local(): pl.pallas_call(scan_kernel, grid=(steps,), in_specs=[back, back, back, ro...  4.68 us
    pallas_call x1, Pallas kernels, local(): pl.pallas_call(functools.partial(finish_kernel, slots=slots, pairs=pairs,...  4.34 us
    pallas_call x1, Pallas kernels, local(): pl.pallas_call(functools.partial(pair_kernel, slots=slots, copies=devices...  1.51 us
    unnamed x2, local copies, waits for them, and re-layouts  0.6 us
  transfers between devices with their start and end apart: 1, of which 1 were waited for; matrix products, arithmetic and copies ran while one was open for 2% of the time, Pallas kernels for 0%

commit v1 on v0

--- a/solution.py
+++ b/solution.py
@@ -16,9 +16,10 @@
     return jnp.broadcast_to(row, (SUBS, row.shape[1]))
 
 
-def scan_kernel(r_ref, v_ref, d_ref, dh_ref, th_ref, g_ref, p_ref, tot_ref, carry, acc):
+def scan_kernel(r_ref, v_ref, d_ref, boot_ref, dh_ref, th_ref, g_ref, p_ref, h_ref, tot_ref, carry, acc):
     step = pl.program_id(0)
     rows, width = r_ref.shape
+    first = (pl.num_programs(0) - 1 - step) * rows
 
     @pl.when(step == 0)
     def _():
@@ -49,8 +50,10 @@
             p = a * p_in
             z_in = spread(u[0:1]) + spread(a[0:1]) * z_in
             p_in = spread(a[0:1]) * p_in
-            g_ref[rs, at] = g
-            p_ref[rs, at] = p
+            to = pl.ds(pl.multiple_of(first + j * SUBS, SUBS), SUBS)
+            g_ref[to, at] = g
+            p_ref[to, at] = p
+            h_ref[to, at] = g + v
             sums = [sums[0] + p, sums[1] + g * p, sums[2] + p * p, sums[3] + g, sums[4] + g * g]
         carry[0, :, at] = z_in
         carry[1, :, at] = p_in
@@ -63,10 +66,10 @@
         tot_ref[1:2] = carry[0, 0:1]
         for i in range(5):
             tot_ref[2 + i:3 + i] = jnp.sum(acc[i], axis=0, keepdims=True)
-        tot_ref[7:8] = jnp.zeros((1, width), F32)
-
-
-def pair_kernel(at_ref, mine_ref, other_ref, boot_ref, th_ref, send_ref, aux_ref, *, slots, copies):
+        tot_ref[7:8] = boot_ref[...] / (1.0 - 1.0 / th_ref[...])
+
+
+def pair_kernel(at_ref, mine_ref, other_ref, send_ref, aux_ref, *, slots, copies):
     width = mine_ref.shape[1]
     half = width // 2
     m = half // LANES
@@ -83,7 +86,7 @@
     pp = lpp + epp * la * la
     g = lg + eg + ep * lz
     gg = lgg + egg + (2.0 * egp + epp * lz) * lz
-    known = boot_ref[...] / (1.0 - 1.0 / th_ref[...])
+    known = mine[7:8]
     is_last = last == 1
     g_end = g + p * known
     gg_end = gg + (2.0 * gp + pp * known) * known
@@ -114,9 +117,10 @@
     send_ref[...] = jnp.broadcast_to(block[None], (copies,) + block.shape)
 
 
-def finish_kernel(at_ref, got_ref, aux_ref, v_ref, g_ref, p_ref, norm_ref, ret_ref, z_ref, st_ref,
+def finish_kernel(at_ref, got_ref, aux_ref, h_ref, g_ref, p_ref, norm_ref, ret_ref, z_ref, st_ref,
                   *, slots, pairs, groups, cells):
-    rows, width = v_ref.shape
+    rows, width = norm_ref.shape
+    first = pl.program_id(0) * rows
     half = width // 2
     m = half // LANES
 
@@ -159,9 +163,10 @@
         z_in = z_ref[:, at]
         for j in range(rows // SUBS):
             rs = pl.ds(j * SUBS, SUBS)
-            adv = g_ref[rs, at] + p_ref[rs, at] * z_in
-            norm_ref[rs, at] = (adv - mean) * scale
-            ret_ref[rs, at] = adv + v_ref[rs, at]
+            of = pl.ds(pl.multiple_of(first + j * SUBS, SUBS), SUBS)
+            lift = p_ref[of, at] * z_in
+            norm_ref[rs, at] = (g_ref[of, at] + lift - mean) * scale
+            ret_ref[rs, at] = h_ref[of, at] + lift
 
 
 def local(rewards, values, done_flags, bootstrap, discount_horizon, trace_horizon):
@@ -181,40 +186,43 @@
     row = pl.BlockSpec((1, width), lambda i: (0, 0))
     eight = pl.BlockSpec((SUBS, width), lambda i: (0, 0))
     full = jax.ShapeDtypeStruct((rows, width), F32)
-    gain, weight, totals = pl.pallas_call(
+    vmem = pl.BlockSpec(memory_space=pltpu.VMEM)
+    smem = pl.BlockSpec(memory_space=pltpu.SMEM)
+    small = pltpu.CompilerParams(vmem_limit_bytes=16 << 20)
+    gain, weight, level, totals = pl.pallas_call(
         scan_kernel,
         grid=(steps,),
-        in_specs=[back, back, back, row, row],
-        out_specs=[back, back, eight],
-        out_shape=[full, full, jax.ShapeDtypeStruct((SUBS, width), F32)],
+        in_specs=[back, back, back, row, row, row],
+        out_specs=[vmem, vmem, vmem, eight],
+        out_shape=[full, full, full, jax.ShapeDtypeStruct((SUBS, width), F32)],
         scratch_shapes=[pltpu.VMEM((2, SUBS, width), F32), pltpu.VMEM((5, SUBS, width), F32)],
+        compiler_params=small,
         name="scan",
-    )(rewards, values, done_flags, dh, th)
+    )(*(pltpu.with_memory_space_constraint(x, pltpu.HBM) for x in (rewards, values, done_flags, boot, dh, th)))
 
     other = lax.ppermute(totals, "tm", [(i, i ^ 1) for i in range(blocks)])
     packed = slots * m + 2
-    vmem = pl.BlockSpec(memory_space=pltpu.VMEM)
-    smem = pl.BlockSpec(memory_space=pltpu.SMEM)
     send, aux = pl.pallas_call(
         functools.partial(pair_kernel, slots=slots, copies=devices),
-        in_specs=[smem, vmem, vmem, vmem, vmem],
+        in_specs=[smem, vmem, vmem],
         out_specs=[vmem, vmem],
         out_shape=[jax.ShapeDtypeStruct((devices, packed, LANES), F32), jax.ShapeDtypeStruct((SUBS, width), F32)],
+        compiler_params=small,
         name="pair",
-    )(place, totals, other, boot, th)
+    )(place, totals, other)
     got = lax.all_to_all(send, ("tm", "env"), 0, 0, tiled=True)
 
-    whole = pl.BlockSpec((devices, packed, LANES), lambda i: (0, 0, 0))
     return tuple(pl.pallas_call(
         functools.partial(finish_kernel, slots=slots, pairs=pairs, groups=groups,
                           cells=1.0 * rows * width * devices),
         grid=(steps,),
-        in_specs=[smem, whole, eight, fore, fore, fore],
+        in_specs=[smem, vmem, vmem, vmem, vmem, vmem],
         out_specs=[fore, fore],
         out_shape=[full, full],
         scratch_shapes=[pltpu.VMEM((SUBS, width), F32), pltpu.VMEM((2, SUBS, LANES), F32)],
+        compiler_params=small,
         name="finish",
-    )(place, got, aux, values, gain, weight))
+    )(place, got, aux, level, gain, weight))
 
 
 def solution(mesh):

time: 28.8 us -> 23.9 us (0.83)
  Pallas kernels: 10.5 us -> 6.87 us
  local copies, waits for them, and re-layouts: 0.6 us -> 0 us
  other arithmetic: 0.56 us -> 0.08 us
  blocking collectives: 15.1 us -> 14.8 us
    pallas_call x1, Pallas kernels: 4.34 us -> 2.63 us  [local(): pl.pallas_call(functools.partial(finish_kernel, slots=slots, pairs=pairs,...]
    pallas_call x1, Pallas kernels: 4.68 us -> 3.64 us  [local(): pl.pallas_call(scan_kernel, grid=(steps,), in_specs=[back, back, back, ro...]
    pallas_call x1, Pallas kernels: 1.51 us -> 0.59 us  [local(): pl.pallas_call(functools.partial(pair_kernel, slots=slots, copies=devices...]
    unnamed x2 -> x0, local copies, waits for them, and re-layouts: 0.6 us -> none
    another operation x1, other arithmetic: 0.56 us -> 0.08 us  [local(): jnp.stack([block_at % 2, (block_at // 2 == pairs - 1).astype(jnp.int32),...]
    all_to_all x1, blocking collectives: 15.1 us -> 14.8 us  [local(): got = lax.all_to_all(send, ('tm', 'env'), 0, 0, tiled=True)]
  transfers between devices with their start and end apart: 1 -> 1, of which waited for: 1 -> 1; matrix products, arithmetic and copies ran while one was open for 2% -> 0% of each run, Pallas kernels for 0% -> 0%
where the time goes in v1:
time: 23.9 us; the launch traced here: 23.7 us
  blocking collectives  14.8 us (62%)
  Pallas kernels  6.87 us (29%)
  waiting for transfers between devices  0.76 us (3%)
  between operations  0.65 us (3%)
  starting transfers between devices  0.56 us (2%)
    all_to_all x1, blocking collectives, local(): got = lax.all_to_all(send, ('tm', 'env'), 0, 0, tiled=True)  14.8 us
    pallas_call x1, Pallas kernels, local(): pl.pallas_call(scan_kernel, grid=(steps,), in_specs=[back, back, back, ro...  3.64 us
    pallas_call x1, Pallas kernels, local(): pl.pallas_call(functools.partial(finish_kernel, slots=slots, pairs=pairs,...  2.63 us
    ppermute x1, waiting for transfers between devices, local(): other = lax.ppermute(totals, 'tm', [(i, i ^ 1) for i in range(blocks)])  0.76 us
    pallas_call x1, Pallas kernels, local(): pl.pallas_call(functools.partial(pair_kernel, slots=slots, copies=devices...  0.59 us
    ppermute x1, starting transfers between devices, local(): other = lax.ppermute(totals, 'tm', [(i, i ^ 1) for i in range(blocks)])  0.56 us
  transfers between devices with their start and end apart: 1, of which 1 were waited for; matrix products, arithmetic and copies ran while one was open for 0% of the time, Pallas kernels for 0%

profile of v1, /device:TPU:0, one launch (start us, length us, event | category | flops | bytes accessed | tf_op | source)
XLA Modules:
  0.0 23.7 jit_solution(17341782670073236900)
XLA Ops:
  0.6 3.6 %scan.1 = (f32[512,512]{1,0:T(8,128)S(1)}, f32[512,512]{1,0:T(8,128)S(1)}, f32[512,512]{1,0:T(8,128)S(1)}, f32[8,512]{1,0:T(8,128)S(1)}) custom-call(f32[512,512]{1,0:T(8,128)} %r_ref.1, f32[512,512]{1,0:T(8,128)} %v_ref.1, s32[512,512]{1,0:T(8,128)} %d_ref.1, f32[1,512]{1,0:T(1,128)} %bitcast.7, f32[1,512]{1,0:T(1,128)} %bitcast.8, f32[1,512]{1,0:T(1,128)} %bitcast.9), custom_call_target="tpu_custom_call" | custom-call | tf_op jit(solution)/shard_map/scan/pallas_call | solution.py:192
  4.3 0.6 %collective-permute-start = (f32[8,512]{1,0:T(8,128)S(1)}, f32[8,512]{1,0:T(8,128)S(1)}, u32[]{:S(2)}, u32[]{:S(2)}) collective-permute-start(f32[8,512]{1,0:T(8,128)S(1)} %get-tuple-element.8.mine_ref), channel_id=1, source_target_pairs={{0,8},{8,0},{16,24},{24,16},{1,9},{9,1},{17,25},{25,17},{2,10},{10... | collective-permute-start | bytes 49160 | tf_op jit(solution)/shard_map/ppermute | solution.py:203
  4.8 0.1 pad_add_fusion.at_ref
  4.9 0.8 %collective-permute-done.other_ref = f32[8,512]{1,0:T(8,128)S(1)} collective-permute-done((f32[8,512]{1,0:T(8,128)S(1)}, f32[8,512]{1,0:T(8,128)S(1)}, u32[]{:S(2)}, u32[]{:S(2)}) %collective-permute-start) | collective-permute-done | bytes 16416 | tf_op jit(solution)/shard_map/ppermute | solution.py:203
  5.7 0.6 %pair.1 = (f32[32,8,128]{2,1,0:T(8,128)S(1)}, f32[8,512]{1,0:T(8,128)S(1)}) custom-call(s32[4]{0:T(128)S(1)} %pad_add_fusion.at_ref, f32[8,512]{1,0:T(8,128)S(1)} %get-tuple-element.8.mine_ref, f32[8,512]{1,0:T(8,128)S(1)} %collective-permute-done.other_ref), custom_call_target="tpu_custom_call" | custom-call | tf_op jit(solution)/shard_map/pair/pallas_call | solution.py:205
  6.3 14.8 %all_to_all.5.got_ref = f32[32,8,128]{2,1,0:T(8,128)S(1)} all-to-all(f32[32,8,128]{2,1,0:T(8,128)S(1)} %get-tuple-element.9), channel_id=1, replica_groups=mesh['tm'=4,'env'=8] {'tm','env'}, dimensions={0} | all-to-all | bytes 262144 | tf_op jit(solution)/shard_map/all_to_all | solution.py:213
  21.1 2.6 %finish.1 = (f32[512,512]{1,0:T(8,128)}, f32[512,512]{1,0:T(8,128)}) custom-call(s32[4]{0:T(128)S(1)} %pad_add_fusion.at_ref, f32[32,8,128]{2,1,0:T(8,128)S(1)} %all_to_all.5.got_ref, f32[8,512]{1,0:T(8,128)S(1)} %get-tuple-element.10.aux_ref, f32[512,512]{1,0:T(8,128)S(1)} %get-tuple-element.11.h_ref, f32[512,512]{1,0:T(8,128)S(1)} %get-tuple-element.12.g_ref, ...), custom_call_target="tpu_custom_call" | custom-call | tf_op jit(solution)/shard_map/finish/pallas_call | solution.py:215
Async XLA Ops:
  4.3 1.4 %collective-permute-start = (f32[8,512]{1,0:T(8,128)S(1)}, f32[8,512]{1,0:T(8,128)S(1)}, u32[]{:S(2)}, u32[]{:S(2)}) collective-permute-start(f32[8,512]{1,0:T(8,128)S(1)} %get-tuple-element.8.mine_ref), channel_id=1, source_target_pairs={{0,8},{8,0},{16,24},{24,16},{1,9},{9,1},{17,25},{25,17},{2,10},{10... | collective-permute-start | bytes 49160 | tf_op jit(solution)/shard_map/ppermute | solution.py:203

commit v2 on v1

v2 whole, which is shorter than its diff:
```python
import functools

import jax
import jax.numpy as jnp
from jax import lax
from jax.experimental import pallas as pl
from jax.experimental.pallas import tpu as pltpu
from jax.sharding import PartitionSpec as P

LANES = 128
SIDE = 1
SUBS = 8
F32 = jnp.float32


def spread(row):
    return jnp.broadcast_to(row, (SUBS, row.shape[1]))


def scan_kernel(r_hbm, v_hbm, d_hbm, boot_hbm, dh_hbm, th_hbm, g_ref, p_ref, v_ref, tot_ref,
                r_ref, d_ref, row_ref, carry, acc, sems, row_sems, *, part):
    rows, width = r_ref.shape
    count = rows // part
    row_copies = [pltpu.make_async_copy(x, row_ref.at[pl.ds(i, 1)], row_sems.at[i])
                  for i, x in enumerate((dh_hbm, th_hbm, boot_hbm))]
    for copy in row_copies:
        copy.start()

    def copies(n):
        at = pl.ds(pl.multiple_of(n * part, part), part)
        return [pltpu.make_async_copy(x.at[at], y.at[at], sems.at[i, n])
                for i, (x, y) in enumerate(((r_hbm, r_ref), (v_hbm, v_ref), (d_hbm, d_ref)))]

    for n in reversed(range(count)):
        for copy in copies(n):
            copy.start()
    carry[0] = jnp.zeros((SUBS, width), F32)
    carry[1] = jnp.ones((SUBS, width), F32)
    acc[...] = jnp.zeros(acc.shape, F32)
    sub = lax.broadcasted_iota(jnp.int32, (SUBS, LANES), 0)
    masks = {k: sub < SUBS - k for k in (1, 2, 4)}
    for copy in row_copies:
        copy.wait()

    def body(i, _):
        n = count - 1 - i
        for copy in copies(n):
            copy.wait()
        for first in range(0, width // LANES, SIDE):
            span = [pl.ds(c * LANES, LANES) for c in range(first, min(first + SIDE, width // LANES))]
            state = []
            for at in span:
                trace = 1.0 - 1.0 / row_ref[1:2, at]
                rate = (1.0 - 1.0 / row_ref[0:1, at]) * trace
                inv = 1.0 / trace
                state.append([spread(rate), spread(inv), spread(inv - 1.0), carry[0, :, at], carry[1, :, at],
                              [acc[i, :, at] for i in range(5)]])
            for j in reversed(range(part // SUBS)):
                rs = pl.ds(pl.multiple_of(n * part + j * SUBS, SUBS), SUBS)
                for b, at in enumerate(span):
                    rate, inv, extra, z_in, p_in, sums = state[b]
                    v = v_ref[rs, at]
                    u = r_ref[rs, at] + v * extra
                    a = jnp.where(d_ref[rs, at] != 0, 0.0, rate)
                    for k in (1, 2, 4):
                        m = masks[k]
                        u = u + jnp.where(m, a, 0.0) * pltpu.roll(u, SUBS - k, 0)
                        a = a * jnp.where(m, pltpu.roll(a, SUBS - k, 0), 1.0)
                    g = u + a * z_in - v * inv
                    p = a * p_in
                    z_in = spread(u[0:1]) + spread(a[0:1]) * z_in
                    p_in = spread(a[0:1]) * p_in
                    g_ref[rs, at] = g
                    p_ref[rs, at] = p
                    sums = [sums[0] + p, sums[1] + g * p, sums[2] + p * p, sums[3] + g, sums[4] + g * g]
                    state[b] = [rate, inv, extra, z_in, p_in, sums]
            for at, (_, _, _, z_in, p_in, sums) in zip(span, state):
                carry[0, :, at] = z_in
                carry[1, :, at] = p_in
                for i in range(5):
                    acc[i, :, at] = sums[i]
        return 0

    lax.fori_loop(0, count, body, 0)
    tot_ref[0:1] = carry[1, 0:1]
    tot_ref[1:2] = carry[0, 0:1]
    for i in range(5):
        tot_ref[2 + i:3 + i] = jnp.sum(acc[i], axis=0, keepdims=True)
    tot_ref[7:8] = row_ref[2:3] / (1.0 - 1.0 / row_ref[1:2])


def pair_kernel(at_ref, mine_ref, other_ref, send_ref, aux_ref, *, slots, copies):
    width = mine_ref.shape[1]
    half = width // 2
    m = half // LANES
    odd, last = at_ref[0], at_ref[1]
    late_here = odd == 1
    mine, other = mine_ref[...], other_ref[...]
    late = jnp.where(late_here, mine, other)
    early = jnp.where(late_here, other, mine)
    la, lz, lp, lgp, lpp, lg, lgg = [late[i:i + 1] for i in range(7)]
    ea, ez, ep, egp, epp, eg, egg = [early[i:i + 1] for i in range(7)]
    a, z = la * ea, ez + ea * lz
    p = lp + ep * la
    gp = lgp + (egp + epp * lz) * la
    pp = lpp + epp * la * la
    g = lg + eg + ep * lz
    gg = lgg + egg + (2.0 * egp + epp * lz) * lz
    known = mine[7:8]
    is_last = last == 1
    g_end = g + p * known
    gg_end = gg + (2.0 * gp + pp * known) * known
    z_end = z + a * known
    g = jnp.where(is_last, g_end, g)
    gg = jnp.where(is_last, gg_end, gg)
    if slots == 3:
        parts = [jnp.where(is_last, z_end, p), gp, pp]
    else:
        parts = [jnp.where(is_last, z_end, z), p, gp, pp, a]
    mult = jnp.where(late_here, jnp.ones_like(la), la)
    add = jnp.where(late_here, jnp.zeros_like(la), lz)
    aux_ref[0:1] = jnp.where(is_last, 0.0, mult)
    aux_ref[1:2] = jnp.where(is_last, add + mult * known, add)
    aux_ref[2:8] = jnp.zeros((6, width), F32)

    def own(x):
        return jnp.where(late_here, x[:, half:], x[:, :half])

    rows = []
    for part in parts:
        h = own(part)
        rows += [h[:, i * LANES:(i + 1) * LANES] for i in range(m)]
    for total in (g, gg):
        h = own(total)
        rows.append(sum(h[:, i * LANES:(i + 1) * LANES] for i in range(m)))
    block = jnp.concatenate(rows, axis=0)
    send_ref[...] = jnp.broadcast_to(block[None], (copies,) + block.shape)


def finish_kernel(at_ref, got_ref, aux_ref, v_ref, g_ref, p_ref, norm_hbm, ret_hbm, norm_ref, ret_ref, sems,
                  *, slots, pairs, groups, cells, part):
    rows, width = norm_ref.shape
    half = width // 2
    m = half // LANES
    count = rows // part

    pair, group = at_ref[2], at_ref[3]
    n = 2 * groups
    base = slots * m
    got = [got_ref[k * n:(k + 1) * n] for k in range(pairs)]
    s1 = sum(jnp.sum(x[:, base:base + 1], axis=0) for x in got)
    s2 = sum(jnp.sum(x[:, base + 1:base + 2], axis=0) for x in got)
    off = 0 if slots == 3 else m
    z = got[pairs - 1][:, 0:m]
    here = [got_ref[(pairs - 1) * n + core * groups + group, 0:m] for core in range(2)]
    pick = here
    for k in reversed(range(pairs - 1)):
        x = got[k]
        p, gp, pp = [x[:, off + i * m:off + (i + 1) * m] for i in range(3)]
        t1 = jnp.sum(p * z, axis=0)
        t2 = jnp.sum((2.0 * gp + pp * z) * z, axis=0)
        s1 = s1 + jnp.sum(t1, axis=0, keepdims=True)
        s2 = s2 + jnp.sum(t2, axis=0, keepdims=True)
        pick = [jnp.where(pair == k, b, a) for a, b in zip(pick, here)]
        if k:
            z = x[:, 0:m] + x[:, 4 * m:5 * m] * z
            nxt = [got_ref[k * n + core * groups + group] for core in range(2)]
            here = [y[0:m] + y[4 * m:5 * m] * h for y, h in zip(nxt, here)]
    flat = jnp.concatenate([h[i:i + 1] for h in pick for i in range(m)], axis=1)
    z_in = aux_ref[1:2] + aux_ref[0:1] * flat
    mean = jnp.sum(s1, axis=1, keepdims=True) / cells
    var = jnp.sum(s2, axis=1, keepdims=True) / cells - mean * mean
    scale = 1.0 / jnp.sqrt(var + 1.0)
    mean = jnp.broadcast_to(mean, (SUBS, LANES))
    scale = jnp.broadcast_to(scale, (SUBS, LANES))

    def copy(n, i):
        at = pl.ds(n * part, part)
        x, y = ((ret_ref, ret_hbm), (norm_ref, norm_hbm))[i]
        return pltpu.make_async_copy(x.at[at], y.at[at], sems.at[i, n])

    def tiles(n):
        for c in range(width // LANES):
            at = pl.ds(c * LANES, LANES)
            z = spread(z_in[:, c * LANES:(c + 1) * LANES])
            for j in range(part // SUBS):
                rs = pl.ds(n * part + j * SUBS, SUBS)
                yield rs, at, g_ref[rs, at] + p_ref[rs, at] * z

    for n in range(count):
        for rs, at, adv in tiles(n):
            ret_ref[rs, at] = adv + v_ref[rs, at]
        copy(n, 0).start()
    for n in range(count):
        for rs, at, adv in tiles(n):
            norm_ref[rs, at] = (adv - mean) * scale
        copy(n, 1).start()
    for n in range(count):
        copy(n, 0).wait()
    for n in range(count):
        copy(n, 1).wait()


def local(rewards, values, done_flags, bootstrap, discount_horizon, trace_horizon):
    rows, width = rewards.shape
    blocks, groups = lax.axis_size("tm"), lax.axis_size("env")
    pairs, devices = blocks // 2, blocks * groups
    slots = 3 if pairs == 2 else 5
    m = width // 2 // LANES
    block_at, group = lax.axis_index("tm"), lax.axis_index("env")
    place = jnp.stack([block_at % 2, (block_at // 2 == pairs - 1).astype(jnp.int32), block_at // 2, group]).astype(jnp.int32)
    boot, dh, th = bootstrap[None], discount_horizon[None], trace_horizon[None]

    part = max(SUBS, rows // 2)
    count = rows // part
    out_part = max(SUBS, rows // 4)
    vmem = pl.BlockSpec(memory_space=pltpu.VMEM)
    smem = pl.BlockSpec(memory_space=pltpu.SMEM)
    hbm = pl.BlockSpec(memory_space=pltpu.HBM)
    small = pltpu.CompilerParams(vmem_limit_bytes=16 << 20)
    full = jax.ShapeDtypeStruct((rows, width), F32)
    gain, weight, kept, totals = pl.pallas_call(
        functools.partial(scan_kernel, part=part),
        in_specs=[hbm] * 6,
        out_specs=[vmem] * 4,
        out_shape=[full, full, full, jax.ShapeDtypeStruct((SUBS, width), F32)],
        scratch_shapes=[
            pltpu.VMEM((rows, width), F32), pltpu.VMEM((rows, width), jnp.int32), pltpu.VMEM((SUBS, width), F32),
            pltpu.VMEM((2, SUBS, width), F32), pltpu.VMEM((5, SUBS, width), F32),
            pltpu.SemaphoreType.DMA((3, count)), pltpu.SemaphoreType.DMA((3,)),
        ],
        compiler_params=small,
        name="scan",
    )(*(pltpu.with_memory_space_constraint(x, pltpu.HBM)
        for x in (rewards, values, done_flags, boot, dh, th)))

    other = lax.ppermute(totals, "tm", [(i, i ^ 1) for i in range(blocks)])
    packed = slots * m + 2
    send, aux = pl.pallas_call(
        functools.partial(pair_kernel, slots=slots, copies=devices),
        in_specs=[smem, vmem, vmem],
        out_specs=[vmem, vmem],
        out_shape=[jax.ShapeDtypeStruct((devices, packed, LANES), F32), jax.ShapeDtypeStruct((SUBS, width), F32)],
        compiler_params=small,
        name="pair",
    )(place, totals, other)
    got = lax.all_to_all(send, ("tm", "env"), 0, 0, tiled=True)

    return tuple(pl.pallas_call(
        functools.partial(finish_kernel, slots=slots, pairs=pairs, groups=groups,
                          cells=1.0 * rows * width * devices, part=out_part),
        in_specs=[smem, vmem, vmem, vmem, vmem, vmem],
        out_specs=[hbm, hbm],
        out_shape=[full, full],
        scratch_shapes=[pltpu.VMEM((rows, width), F32), pltpu.VMEM((rows, width), F32),
                        pltpu.SemaphoreType.DMA((2, rows // out_part))],
        compiler_params=small,
        name="finish",
    )(place, got, aux, kept, gain, weight))


def solution(mesh):
    placed = (P("tm", "env"), P("tm", "env"), P("tm", "env"), P("env"), P("env"), P("env"))
    return jax.shard_map(
        local,
        mesh=mesh,
        in_specs=placed,
        out_specs=(P("tm", "env"), P("tm", "env")),
        check_vma=False,
    )
```

time: 23.9 us -> 22.9 us (0.958)
  Pallas kernels: 6.87 us -> 5.85 us
    pallas_call x1, Pallas kernels: 2.63 us -> 2.03 us  [local(): pl.pallas_call(functools.partial(finish_kernel, slots=slots, pairs=pairs,...]
    pallas_call x1, Pallas kernels: 3.64 us -> 3.23 us  [local(): pl.pallas_call(functools.partial(scan_kernel, part=part), in_specs=[hbm]...]
where the time goes in v2:
time: 22.9 us; the launch traced here: 22.7 us
  blocking collectives  14.8 us (65%)
  Pallas kernels  5.85 us (26%)
  waiting for transfers between devices  0.76 us (3%)
  between operations  0.65 us (3%)
  starting transfers between devices  0.56 us (2%)
    all_to_all x1, blocking collectives, local(): got = lax.all_to_all(send, ('tm', 'env'), 0, 0, tiled=True)  14.8 us
    pallas_call x1, Pallas kernels, local(): pl.pallas_call(functools.partial(scan_kernel, part=part), in_specs=[hbm]...  3.23 us
    pallas_call x1, Pallas kernels, local(): pl.pallas_call(functools.partial(finish_kernel, slots=slots, pairs=pairs,...  2.03 us
    ppermute x1, waiting for transfers between devices, local(): other = lax.ppermute(totals, 'tm', [(i, i ^ 1) for i in range(blocks)])  0.76 us
    pallas_call x1, Pallas kernels, local(): pl.pallas_call(functools.partial(pair_kernel, slots=slots, copies=devices...  0.59 us
    ppermute x1, starting transfers between devices, local(): other = lax.ppermute(totals, 'tm', [(i, i ^ 1) for i in range(blocks)])  0.56 us
  transfers between devices with their start and end apart: 1, of which 1 were waited for; matrix products, arithmetic and copies ran while one was open for 0% of the time, Pallas kernels for 0%

profile of v2, /device:TPU:0, one launch (start us, length us, event | category | flops | bytes accessed | tf_op | source)
XLA Modules:
  0.0 22.7 jit_solution(13153596775342536646)
XLA Ops:
  0.6 3.2 %scan.1 = (f32[512,512]{1,0:T(8,128)S(1)}, f32[512,512]{1,0:T(8,128)S(1)}, f32[512,512]{1,0:T(8,128)S(1)}, f32[8,512]{1,0:T(8,128)S(1)}) custom-call(f32[512,512]{1,0:T(8,128)} %r_hbm.1, f32[512,512]{1,0:T(8,128)} %v_hbm.1, s32[512,512]{1,0:T(8,128)} %d_hbm.1, f32[1,512]{1,0:T(1,128)} %bitcast.7, f32[1,512]{1,0:T(1,128)} %bitcast.8, f32[1,512]{1,0:T(1,128)} %bitcast.9), custom_call_target="tpu_custom_call" | custom-call | tf_op jit(solution)/shard_map/scan/pallas_call | solution.py:222
  3.9 0.6 %collective-permute-start = (f32[8,512]{1,0:T(8,128)S(1)}, f32[8,512]{1,0:T(8,128)S(1)}, u32[]{:S(2)}, u32[]{:S(2)}) collective-permute-start(f32[8,512]{1,0:T(8,128)S(1)} %get-tuple-element.8.mine_ref), channel_id=1, source_target_pairs={{0,8},{8,0},{16,24},{24,16},{1,9},{9,1},{17,25},{25,17},{2,10},{10... | collective-permute-start | bytes 49160 | tf_op jit(solution)/shard_map/ppermute | solution.py:237
  4.4 0.1 pad_add_fusion.at_ref
  4.5 0.8 %collective-permute-done.other_ref = f32[8,512]{1,0:T(8,128)S(1)} collective-permute-done((f32[8,512]{1,0:T(8,128)S(1)}, f32[8,512]{1,0:T(8,128)S(1)}, u32[]{:S(2)}, u32[]{:S(2)}) %collective-permute-start) | collective-permute-done | bytes 16416 | tf_op jit(solution)/shard_map/ppermute | solution.py:237
  5.3 0.6 %pair.1 = (f32[32,8,128]{2,1,0:T(8,128)S(1)}, f32[8,512]{1,0:T(8,128)S(1)}) custom-call(s32[4]{0:T(128)S(1)} %pad_add_fusion.at_ref, f32[8,512]{1,0:T(8,128)S(1)} %get-tuple-element.8.mine_ref, f32[8,512]{1,0:T(8,128)S(1)} %collective-permute-done.other_ref), custom_call_target="tpu_custom_call" | custom-call | tf_op jit(solution)/shard_map/pair/pallas_call | solution.py:239
  5.9 14.8 %all_to_all.5.got_ref = f32[32,8,128]{2,1,0:T(8,128)S(1)} all-to-all(f32[32,8,128]{2,1,0:T(8,128)S(1)} %get-tuple-element.9), channel_id=1, replica_groups=mesh['tm'=4,'env'=8] {'tm','env'}, dimensions={0} | all-to-all | bytes 262144 | tf_op jit(solution)/shard_map/all_to_all | solution.py:247
  20.7 2.0 %finish.1 = (f32[512,512]{1,0:T(8,128)}, f32[512,512]{1,0:T(8,128)}) custom-call(s32[4]{0:T(128)S(1)} %pad_add_fusion.at_ref, f32[32,8,128]{2,1,0:T(8,128)S(1)} %all_to_all.5.got_ref, f32[8,512]{1,0:T(8,128)S(1)} %get-tuple-element.10.aux_ref, f32[512,512]{1,0:T(8,128)S(1)} %get-tuple-element.11.v_ref, f32[512,512]{1,0:T(8,128)S(1)} %get-tuple-element.12.g_ref, ...), custom_call_target="tpu_custom_call" | custom-call | tf_op jit(solution)/shard_map/finish/pallas_call | solution.py:249
Async XLA Ops:
  3.9 1.4 %collective-permute-start = (f32[8,512]{1,0:T(8,128)S(1)}, f32[8,512]{1,0:T(8,128)S(1)}, u32[]{:S(2)}, u32[]{:S(2)}) collective-permute-start(f32[8,512]{1,0:T(8,128)S(1)} %get-tuple-element.8.mine_ref), channel_id=1, source_target_pairs={{0,8},{8,0},{16,24},{24,16},{1,9},{9,1},{17,25},{25,17},{2,10},{10... | collective-permute-start | bytes 49160 | tf_op jit(solution)/shard_map/ppermute | solution.py:237
